TPU v7x, 256 devices: a whole 4x4x8 slice. The times are simulated.
256 devices in a mesh: row: 16 (over z_hi, y), col: 16 (over z_lo, x, core).
Axes of the slice: x: 4, y: 4, z: 8 (z_hi: 4, z_lo: 2; z = z_hi * 2 + z_lo), core: 2. Of those that a mesh axis runs over, the one named last changes fastest.
Arguments:
- tokens: bfloat16 [8192, 4096], P('row', 'col'), may hold values from -6 to 6
- norm_gain: bfloat16 [4096], P('col'), may hold values from 0.099609375 to 1.8984375
- gate_weight: bfloat16 [4096, 10240], P('row', 'col'), may hold values from -0.09375 to 0.09375
- linear_weight: bfloat16 [4096, 10240], P('row', 'col'), may hold values from -0.09375 to 0.09375
- output_weight: bfloat16 [10240, 4096], P('col', 'row'), may hold values from -0.078125 to 0.078125
Outputs:
- block_out: bfloat16 [8192, 4096], P('row', 'col')
All inputs are finite; a program needn't handle non-finite values.
Results may differ from a plain program's by a relative error of at most 0.0065.
Values may be sent and summed in bfloat16 or wider, within the bound.
A program may use at most 128 MiB of HBM per device.

v0:
```python
import jax
import jax.numpy as jnp
from jax import lax
from jax.sharding import PartitionSpec as P


def turned_gather(arrays, axis, dims):
    turned = [jnp.moveaxis(a, dim, 0) for a, dim in zip(arrays, dims)]
    widths = [t[0].size for t in turned]
    both = jnp.concatenate([t.reshape(-1, w) for t, w in zip(turned, widths)], axis=1)
    filled = lax.all_gather(both, axis, axis=0, tiled=True)
    parts = jnp.split(filled, [sum(widths[:k]) for k in range(1, len(widths))], axis=1)
    return tuple(
        (
            jnp.moveaxis(b.reshape(-1, *t.shape[1:]), 0, dim)
            for b, t, dim in zip(parts, turned, dims)
        )
    )


def side_by_side(arrays, axis, dim, along):
    both = jnp.concatenate(arrays, axis=along)
    filled, at, gathered = (lax.all_gather(both, axis, axis=dim, tiled=True), 0, [])
    for a in arrays:
        gathered.append(lax.slice_in_dim(filled, at, at + a.shape[along], axis=along))
        at += a.shape[along]
    return tuple(gathered)


def add_rows(left, piece):
    return jnp.dot(left, piece, preferred_element_type=jnp.float32)


def local(tokens, norm_gain, gate_weight, linear_weight, output_weight):
    whole, gain_all = turned_gather((tokens, norm_gain), "col", (1, 0))
    values = whole.astype(jnp.float32)
    meansq = jnp.mean(values * values, axis=-1, keepdims=True)
    normed = (values * lax.rsqrt(meansq + 1e-06) * gain_all.astype(jnp.float32)).astype(
        jnp.bfloat16
    )
    pieces = side_by_side((gate_weight, linear_weight), "row", 0, 1)
    gate = add_rows(normed, pieces[0])
    linear = add_rows(normed, pieces[1])
    hidden = (jax.nn.gelu(gate, approximate=True) * linear).astype(jnp.bfloat16)
    terms = jnp.dot(
        hidden,
        lax.all_gather(output_weight, "row", axis=1, tiled=True),
        preferred_element_type=jnp.float32,
    )
    return lax.psum_scatter(terms, "col", scatter_dimension=1, tiled=True).astype(jnp.bfloat16)


def solution(mesh):
    return jax.shard_map(
        local,
        mesh=mesh,
        in_specs=(P("row", "col"), P("col"), P("row", "col"), P("row", "col"), P("col", "row")),
        out_specs=P("row", "col"),
        check_vma=False,
    )
```

profile of v0, /device:TPU:8, one launch (start us, length us, event | category | flops | bytes accessed | tf_op | source)
XLA Modules:
  0.0 385.9 jit_solution(17165300564856851926)
XLA Ops:
  6.5 0.0 all-gather.4.cloned.1.call-start
  6.5 0.7 reshape.19
  7.2 1.7 pad_maximum_fusion.1
  8.9 0.0 all-gather.4.cloned.1.call-update
  8.9 0.0 all-gather.6.cloned.1.call-start
  8.9 2.0 pad_maximum_fusion
  10.9 0.0 all-gather.6.cloned.1.call-update
  10.9 0.0 all-gather.8.cloned.1.call-start
  11.0 0.7 all-gather.8.cloned.1.call-update
  11.7 0.0 reduce-scatter.2.cloned.1.call-start
  11.7 48.1 %all-gather.4.cloned.1.call-done = bf16[4096,513]{0,1:T(8,128)(2,1)} async-done(((bf16[256,513]{0,1:T(8,128)(2,1)}), bf16[4096,513]{0,1:T(8,128)(2,1)}) %all-gather.4.cloned.1.call-update) | async-done | bytes 4202512 | tf_op jit(solution)/shard_map/all_gather | solution.py:11
  59.8 0.0 slice-start
  59.8 3.1 fusion
  62.9 0.9 slice_convert_fusion
  63.8 128.5 %all-gather.6.cloned.1.call-done = bf16[4096,1280]{1,0:T(8,128)(2,1)} async-done(((bf16[256,1280]{1,0:T(8,128)(2,1)}), bf16[4096,1280]{1,0:T(8,128)(2,1)}) %all-gather.6.cloned.1.call-update) | async-done | bytes 10485776 | tf_op jit(solution)/shard_map/all_gather | solution.py:23
  192.3 0.0 slice-start.1
  192.3 0.0 copy-start
  192.3 7.1 %fusion.5 = f32[512,640]{1,0:T(8,128)S(1)} fusion(bf16[4096,1280]{1,0:T(8,128)(2,1)} %all-gather.6.cloned.1.call-done, f32[4096]{0:T(1024)S(1)} %bitcast.7, f32[512]{0:T(512)S(1)} %add_rsqrt_fusion, bf16[4096,513]{0,1:T(8,128)(2,1)} %all-gather.4.cloned.1.call-done), kind=kOutput, calls=%fused_computation.7 | convolution fusion | flops 2692743168 | bytes 10766336 | tf_op jit(solution)/shard_map/dot_general | solution.py:31
  199.3 0.0 slice-done
  199.3 0.0 slice-done.1
  199.3 0.9 copy-done
  200.2 3.7 fusion.10
  203.9 87.6 %all-gather.8.cloned.1.call-done = bf16[640,4096]{1,0:T(8,128)(2,1)} async-done(((bf16[640,256]{1,0:T(8,128)(2,1)}), bf16[640,4096]{1,0:T(8,128)(2,1)}) %all-gather.8.cloned.1.call-update) | async-done | bytes 5242896 | tf_op jit(solution)/shard_map/all_gather | solution.py:47
  291.5 8.2 %fusion.22 = f32[512,4096]{1,0:T(8,128)} fusion(bf16[512,640]{1,0:T(8,128)(2,1)S(1)} %fusion.10, bf16[640,4096]{1,0:T(8,128)(2,1)} %all-gather.8.cloned.1.call-done), kind=kOutput, calls=%fused_computation.23 | convolution fusion | flops 2684354560 | bytes 14286848 | tf_op jit(solution)/shard_map/dot_general | solution.py:45
  299.7 0.0 reduce-scatter.2.cloned.1.call-update
  299.7 77.9 %reduce-scatter.2.cloned.1.call-done = f32[512,256]{1,0:T(8,128)} async-done(((f32[512,4096]{1,0:T(8,128)}), f32[512,256]{1,0:T(8,128)}) %reduce-scatter.2.cloned.1.call-update) | async-done | bytes 524304 | tf_op jit(solution)/shard_map/reduce_scatter | solution.py:50
  377.6 1.8 convert_element_type.29
  (2 shorter events, 0.0 us)
Async XLA Ops:
  6.5 53.2 %all-gather.4.cloned.1.call-start = ((), (), s32[]{:S(2)}) async-start(), calls=%async_computation.1 | async-start | bytes 4526080 | tf_op jit(solution)/shard_map/all_gather | solution.py:11
  8.9 183.4 %all-gather.6.cloned.1.call-start = ((), (), s32[]{:S(2)}) async-start(), calls=%async_computation.2 | async-start | bytes 11141120 | tf_op jit(solution)/shard_map/all_gather | solution.py:23
  10.9 280.6 %all-gather.8.cloned.1.call-start = ((), (), s32[]{:S(2)}) async-start(), calls=%async_computation.3 | async-start | bytes 5570560 | tf_op jit(solution)/shard_map/all_gather | solution.py:47
  11.7 365.9 %reduce-scatter.2.cloned.1.call-start = ((), (), s32[]{:S(2)}) async-start(), calls=%async_computation.4 | async-start | bytes 8912896 | tf_op jit(solution)/shard_map/reduce_scatter | solution.py:50
  59.8 139.6 %slice-start = ((s8[4259840]{0:T(1024)(128)(4,1)}), s8[65536]{0:T(1024)(128)(4,1)S(1)}, s32[]{:S(2)}) async-start(s8[4259840]{0:T(1024)(128)(4,1)} %bitcast.4), calls=%async_computation.5 | async-start | bytes 131072
  192.3 7.1 %slice-start.1 = ((s8[4259840]{0:T(1024)(128)(4,1)}), s8[4194304]{0:T(1024)(128)(4,1)S(1)}, s32[]{:S(2)}) async-start(s8[4259840]{0:T(1024)(128)(4,1)} %bitcast.4), calls=%async_computation.6 | async-start | bytes 8388608
  192.3 8.0 %copy-start = (bf16[4096,1280]{1,0:T(8,128)(2,1)S(1)}, bf16[4096,1280]{1,0:T(8,128)(2,1)}, u32[]{:S(2)}) copy-start(bf16[4096,1280]{1,0:T(8,128)(2,1)} %all-gather.6.cloned.1.call-done) | copy-start | bytes 31457284
Sparse Core Ops, SparseCore 0:
  9.1 50.6 all-gather.3
  62.2 130.0 all-gather.5
  194.7 96.7 all-gather.7
  299.8 77.6 reduce-scatter.1
where the time goes:
time: 386 us
  waiting for transfers between devices  343 us (89%)
  matrix products  18.9 us (5%)
  between operations  13.2 us (3%)
  other arithmetic  9.37 us (2%)
    all_gather x1, waiting for transfers between devices, side_by_side(): lax.all_gather(both, axis, axis=dim, tiled=True)  128 us
    all_gather x1, waiting for transfers between devices, local(): lax.all_gather(output_weight, 'row', axis=1, tiled=True)  87.6 us
    reduce_scatter x1, waiting for transfers between devices, local(): lax.psum_scatter(terms, 'col', scatter_dimension=1, tiled=True)  77.9 us
    all_gather x1, waiting for transfers between devices, turned_gather(): filled = lax.all_gather(both, axis, axis=0, tiled=True)  48.1 us
    dot_general x2, matrix products, add_rows(): return jnp.dot(left, piece, preferred_element_type=jnp.float32)  10.7 us
    dot_general x1, matrix products, local(): jnp.dot(hidden, lax.all_gather(output_weight, 'row', axis=1, tiled=True),...  8.15 us
  transfers between devices with their start and end apart: 4, of which 4 were waited for; matrix products, arithmetic and copies ran while one was open for 4% of the time, Pallas kernels for 0%

commit v1 on v0

--- a/solution.py
+++ b/solution.py
@@ -8,7 +8,9 @@
     turned = [jnp.moveaxis(a, dim, 0) for a, dim in zip(arrays, dims)]
     widths = [t[0].size for t in turned]
     both = jnp.concatenate([t.reshape(-1, w) for t, w in zip(turned, widths)], axis=1)
-    filled = lax.all_gather(both, axis, axis=0, tiled=True)
+    filled = jnp.concatenate(
+        lax.all_to_all(jnp.stack([both] * lax.axis_size(axis)), axis, 0, 0), axis=0
+    )
     parts = jnp.split(filled, [sum(widths[:k]) for k in range(1, len(widths))], axis=1)
     return tuple(
         (

time: 386 us -> 365 us (0.946)
  waiting for transfers between devices: 343 us -> 310 us
  local copies, waits for them, and re-layouts: 1.55 us -> 11.3 us
  starting transfers between devices: 0.12 us -> 5.88 us
    all_to_all x0 -> x1, waiting for transfers between devices: none -> 127 us  [turned_gather(): lax.all_to_all(jnp.stack([both] * lax.axis_size(axis)), axis, 0, 0)]
    all_gather x1, waiting for transfers between devices: 128 us -> 26.4 us  [side_by_side(): lax.all_gather(both, axis, axis=dim, tiled=True)]
    all_gather x1 -> x0, waiting for transfers between devices: 48.1 us -> none  [turned_gather(): filled = lax.all_gather(both, axis, axis=0, tiled=True)]
    all_gather x1, waiting for transfers between devices: 87.6 us -> 78 us  [local(): lax.all_gather(output_weight, 'row', axis=1, tiled=True)]
    all_to_all x0 -> x1, starting transfers between devices: none -> 5.8 us  [turned_gather(): lax.all_to_all(jnp.stack([both] * lax.axis_size(axis)), axis, 0, 0)]
    unnamed x6 -> x8, local copies, waits for them, and re-layouts: 0.9 us -> 5.24 us
  transfers between devices with their start and end apart: 4 -> 4, of which waited for: 4 -> 4; matrix products, arithmetic and copies ran while one was open for 4% -> 6% of each run, Pallas kernels for 0% -> 0%
where the time goes in v1:
time: 365 us
  waiting for transfers between devices  310 us (85%)
  matrix products  18.7 us (5%)
  between operations  13.2 us (4%)
  local copies, waits for them, and re-layouts  11.3 us (3%)
  starting transfers between devices  5.88 us (2%)
  other arithmetic  5.61 us (2%)
    all_to_all x1, waiting for transfers between devices, turned_gather(): lax.all_to_all(jnp.stack([both] * lax.axis_size(axis)), axis, 0, 0)  127 us
    all_gather x1, waiting for transfers between devices, local(): lax.all_gather(output_weight, 'row', axis=1, tiled=True)  78 us
    reduce_scatter x1, waiting for transfers between devices, local(): lax.psum_scatter(terms, 'col', scatter_dimension=1, tiled=True)  77.9 us
    all_gather x1, waiting for transfers between devices, side_by_side(): lax.all_gather(both, axis, axis=dim, tiled=True)  26.4 us
    dot_general x2, matrix products, add_rows(): return jnp.dot(left, piece, preferred_element_type=jnp.float32)  10.7 us
    dot_general x1, matrix products, local(): jnp.dot(hidden, lax.all_gather(output_weight, 'row', axis=1, tiled=True),...  8.07 us
  transfers between devices with their start and end apart: 4, of which 4 were waited for; matrix products, arithmetic and copies ran while one was open for 6% of the time, Pallas kernels for 0%

profile of v1, /device:TPU:8, one launch (start us, length us, event | category | flops | bytes accessed | tf_op | source)
XLA Modules:
  0.0 364.7 jit_solution(15707432477719718268)
XLA Ops:
  6.5 0.0 all-gather.3.cloned.1.call-start
  6.5 2.0 pad_maximum_fusion
  8.5 0.0 all-gather.3.cloned.1.call-update
  8.5 0.7 reshape.24
  9.2 1.0 pad_maximum_fusion.1
  10.2 2.3 stack.2
  12.4 5.8 %all-to-all-start = ((bf16[16,256,513]{1,2,0:T(8,128)(2,1)}), bf16[16,256,513]{1,2,0:T(8,128)(2,1)}, u32[]{:S(2)}, u32[]{:S(2)}) async-start(bf16[16,256,513]{1,2,0:T(8,128)(2,1)} %stack.2), calls=%async_computation | async-start | bytes 8519680 | tf_op jit(solution)/shard_map/all_to_all | solution.py:12
  18.2 0.0 all-gather.5.cloned.1.call-start
  18.3 0.7 all-gather.5.cloned.1.call-update
  19.0 0.0 reduce-scatter.2.cloned.1.call-start
  19.0 127.0 %all-to-all-done = bf16[16,256,513]{1,2,0:T(8,128)(2,1)} async-done(((bf16[16,256,513]{1,2,0:T(8,128)(2,1)}), bf16[16,256,513]{1,2,0:T(8,128)(2,1)}, u32[]{:S(2)}, u32[]{:S(2)}) %all-to-all-start) | async-done | bytes 4202528 | tf_op jit(solution)/shard_map/all_to_all | solution.py:12
  146.0 3.1 copy.10
  149.1 0.3 pad.4
  149.4 3.0 copy.8
  152.4 0.0 copy-start
  152.4 0.9 fusion
  153.3 1.0 copy-done
  154.3 26.4 %all-gather.3.cloned.1.call-done = bf16[4096,1280]{1,0:T(8,128)(2,1)} async-done(((bf16[256,1280]{1,0:T(8,128)(2,1)}), bf16[4096,1280]{1,0:T(8,128)(2,1)}) %all-gather.3.cloned.1.call-update) | async-done | bytes 10485776 | tf_op jit(solution)/shard_map/all_gather | solution.py:25
  180.7 0.0 copy-start.1
  180.8 0.0 copy-start.2
  180.8 7.0 %fusion.5 = f32[512,640]{1,0:T(8,128)S(1)} fusion(bf16[4096,1280]{1,0:T(8,128)(2,1)} %all-gather.3.cloned.1.call-done, f32[4096]{0:T(1024)S(1)} %bitcast.18, f32[512]{0:T(512)S(1)} %add_rsqrt_fusion, bf16[4096,513]{0,1:T(8,128)(2,1)} %bitcast.14), kind=kOutput, calls=%fused_computation.7 | convolution fusion | flops 2692743168 | bytes 10766336 | tf_op jit(solution)/shard_map/dot_general | solution.py:33
  187.8 0.0 copy-done.1
  187.8 0.9 copy-done.2
  188.7 3.6 fusion.10
  192.4 78.0 %all-gather.5.cloned.1.call-done = bf16[640,4096]{1,0:T(8,128)(2,1)} async-done(((bf16[640,256]{1,0:T(8,128)(2,1)}), bf16[640,4096]{1,0:T(8,128)(2,1)}) %all-gather.5.cloned.1.call-update) | async-done | bytes 5242896 | tf_op jit(solution)/shard_map/all_gather | solution.py:49
  270.4 8.1 %fusion.22 = f32[512,4096]{1,0:T(8,128)} fusion(bf16[512,640]{1,0:T(8,128)(2,1)S(1)} %fusion.10, bf16[640,4096]{1,0:T(8,128)(2,1)} %all-gather.5.cloned.1.call-done), kind=kOutput, calls=%fused_computation.24 | convolution fusion | flops 2684354560 | bytes 14286848 | tf_op jit(solution)/shard_map/dot_general | solution.py:47
  278.5 0.0 reduce-scatter.2.cloned.1.call-update
  278.5 77.9 %reduce-scatter.2.cloned.1.call-done = f32[512,256]{1,0:T(8,128)} async-done(((f32[512,4096]{1,0:T(8,128)}), f32[512,256]{1,0:T(8,128)}) %reduce-scatter.2.cloned.1.call-update) | async-done | bytes 524304 | tf_op jit(solution)/shard_map/reduce_scatter | solution.py:52
  356.4 1.8 convert_element_type.29
  (2 shorter events, 0.0 us)
Async XLA Ops:
  6.5 174.2 %all-gather.3.cloned.1.call-start = ((), (), s32[]{:S(2)}) async-start(), calls=%async_computation.2 | async-start | bytes 11141120 | tf_op jit(solution)/shard_map/all_gather | solution.py:25
  12.4 133.6 %all-to-all-start = ((bf16[16,256,513]{1,2,0:T(8,128)(2,1)}), bf16[16,256,513]{1,2,0:T(8,128)(2,1)}, u32[]{:S(2)}, u32[]{:S(2)}) async-start(bf16[16,256,513]{1,2,0:T(8,128)(2,1)} %stack.2), calls=%async_computation | async-start | bytes 8519680 | tf_op jit(solution)/shard_map/all_to_all | solution.py:12
  18.2 252.2 %all-gather.5.cloned.1.call-start = ((), (), s32[]{:S(2)}) async-start(), calls=%async_computation.3 | async-start | bytes 5570560 | tf_op jit(solution)/shard_map/all_gather | solution.py:49
  19.0 337.4 %reduce-scatter.2.cloned.1.call-start = ((), (), s32[]{:S(2)}) async-start(), calls=%async_computation.4 | async-start | bytes 8912896 | tf_op jit(solution)/shard_map/reduce_scatter | solution.py:52
  152.4 2.0 copy-start
  180.7 7.1 %copy-start.1 = (bf16[65,8,16,256]{3,1,2,0:T(8,128)(2,1)S(1)}, bf16[65,8,16,256]{3,1,2,0:T(8,128)(2,1)}, u32[]{:S(2)}) copy-start(bf16[65,8,16,256]{3,1,2,0:T(8,128)(2,1)} %copy-done) | copy-start | bytes 12779524
  180.8 8.0 %copy-start.2 = (bf16[4096,1280]{1,0:T(8,128)(2,1)S(1)}, bf16[4096,1280]{1,0:T(8,128)(2,1)}, u32[]{:S(2)}) copy-start(bf16[4096,1280]{1,0:T(8,128)(2,1)} %all-gather.3.cloned.1.call-done) | copy-start | bytes 31457284
Sparse Core Ops, SparseCore 0:
  9.8 170.9 all-gather.2
  183.1 87.2 all-gather.4
  278.6 77.6 reduce-scatter.1
